TPU v7x, 8 devices: a whole 2x2x1 slice. The times are simulated.
8 devices in a mesh: dp: 1 (over z), tp: 2 (over y), ep: 4 (over x, core).
Axes of the slice: x: 2, y: 2, z: 1, core: 2. Of those that a mesh axis runs over, the one named last changes fastest.
Arguments:
- tokens: bfloat16 [256, 2048], P(('dp', 'ep'))
- expert_ids: int32 [256, 8], P(('dp', 'ep'))
- norm_gain: bfloat16 [2048], replicated
- router_w: bfloat16 [2048, 64], replicated
- w_gate: bfloat16 [64, 2048, 1024], P('ep', None, 'tp')
- w_up: bfloat16 [64, 2048, 1024], P('ep', None, 'tp')
- w_down: bfloat16 [64, 1024, 2048], P('ep', 'tp')
Outputs:
- output: bfloat16 [256, 2048], P(('dp', 'ep'))
All inputs are finite; a program needn't handle non-finite values.
Results may differ from a plain program's by a relative error of at most 0.0102047.
Values are sent between devices in bfloat16 or wider.
A program may use at most 1 GiB of HBM per device.

v0:
```python
import jax
import jax.numpy as jnp
from jax import lax
from jax.sharding import PartitionSpec as P

NORM_EPS = 1e-5


def route_local(tokens, expert_ids, norm_gain, router_w):
    num_tok, top_k = expert_ids.shape
    num_exp = router_w.shape[1]
    slot_cap = 2 * top_k * num_tok // num_exp
    tok_f32 = tokens.astype(jnp.float32)
    inv_rms = lax.rsqrt(jnp.mean(tok_f32 * tok_f32, axis=-1, keepdims=True) + NORM_EPS)
    normed = (tok_f32 * inv_rms * norm_gain.astype(jnp.float32)).astype(jnp.bfloat16)
    logits = jnp.dot(normed, router_w, preferred_element_type=jnp.float32)
    gates = jax.nn.softmax(jnp.take_along_axis(logits, expert_ids, axis=1), axis=-1)
    flat_ids = expert_ids.reshape(-1)
    onehot = (flat_ids[:, None] == jnp.arange(num_exp, dtype=jnp.int32)[None, :]).astype(jnp.int32)
    slot_ids = jnp.sum(jnp.cumsum(onehot, axis=0) * onehot, axis=1) - 1
    dest_pos = flat_ids * slot_cap + slot_ids
    row_tok = jnp.arange(num_tok * top_k, dtype=jnp.int32) // top_k
    src_rows = jnp.zeros((num_exp * slot_cap,), jnp.int32).at[dest_pos].set(row_tok)
    return normed, gates, src_rows, dest_pos


def expert_ffn(rows, w_gate, w_up, w_down):
    gate_act = jnp.einsum('ecd,edf->ecf', rows, w_gate, preferred_element_type=jnp.float32)
    up_act = jnp.einsum('ecd,edf->ecf', rows, w_up, preferred_element_type=jnp.float32)
    hidden = (jax.nn.silu(gate_act) * up_act).astype(jnp.bfloat16)
    return jnp.einsum('ecf,efd->ecd', hidden, w_down, preferred_element_type=jnp.float32).astype(jnp.bfloat16)


def solution(mesh):
    ep_size = mesh.shape['ep']
    tok_spec = P(('dp', 'ep'), None)

    def local_block(tokens, expert_ids, norm_gain, router_w, w_gate, w_up, w_down):
        num_tok, model_dim = tokens.shape
        top_k = expert_ids.shape[1]
        num_exp = router_w.shape[1]
        local_exp = num_exp // ep_size
        slot_cap = 2 * top_k * num_tok // num_exp
        normed, gates, src_rows, dest_pos = route_local(tokens, expert_ids, norm_gain, router_w)
        send_buf = normed[src_rows].reshape(ep_size, local_exp, slot_cap, model_dim)
        recv_buf = lax.all_to_all(send_buf, 'ep', 0, 2, tiled=True)
        recv_buf = recv_buf.reshape(local_exp, ep_size * slot_cap, model_dim)
        part_out = expert_ffn(recv_buf, w_gate, w_up, w_down)
        full_out = lax.psum(part_out, 'tp')
        full_out = full_out.reshape(1, local_exp, ep_size * slot_cap, model_dim)
        back_buf = lax.all_to_all(full_out, 'ep', 2, 0, tiled=True)
        back_buf = back_buf.reshape(num_exp * slot_cap, model_dim)
        picked = back_buf[dest_pos].reshape(num_tok, top_k, model_dim).astype(jnp.float32)
        mixed = jnp.sum(gates[:, :, None] * picked, axis=1)
        return (tokens.astype(jnp.float32) + mixed).astype(jnp.bfloat16)

    return jax.shard_map(local_block, mesh=mesh, in_specs=(tok_spec, tok_spec, P(None), P(None, None), P('ep', None, 'tp'), P('ep', None, 'tp'), P('ep', 'tp', None)), out_specs=tok_spec, check_vma=False)
```

profile of v0, /device:TPU:0, one launch (start us, length us, event | category | flops | bytes accessed | tf_op | source)
XLA Modules:
  0.0 304.7 jit_solution(6939815741690575993)
XLA Ops:
  6.5 0.7 broadcast_multiply_fusion
  7.3 0.8 copy.38
  8.0 0.1 eq.29
  8.1 0.1 eq.25
  8.2 1.1 fusion.1
  9.3 0.7 convert_element_type.31
  10.0 0.1 copy.37
  10.1 0.1 mul.61
  10.2 1.2 reduce-window.6
  11.4 0.2 slice_reduce_fusion
  11.7 0.1 fusion.6
  11.9 2.4 scatter_custom_fusion
  14.3 1.1 fusion.3
  15.4 6.0 %gather_fusion = bf16[1024,2048]{1,0:T(8,128)(2,1)} fusion(bf16[64,2048]{1,0:T(8,128)(2,1)S(1)} %fusion.3, s32[1024]{0:T(1024)S(1)} %fusion.8), kind=kCustom, calls=%fused_computation | custom fusion | bytes 8392704 | tf_op jit(solution)/shard_map/gather | solution.py:45
  21.4 52.7 %all_to_all.30 = bf16[4,16,16,2048]{3,2,1,0:T(8,128)(2,1)S(1)} all-to-all(bf16[4,16,16,2048]{3,2,1,0:T(8,128)(2,1)} %bitcast.46), channel_id=1, replica_groups=mesh['dp'=1,'tp'=2,'ep'=4] {'ep'}, dimensions={0} | all-to-all | bytes 8388608 | tf_op jit(solution)/shard_map/all_to_all | solution.py:46
  74.2 2.2 copy.41
  76.4 14.6 %fusion.19 = f32[16,64,512]{2,1,0:T(8,128)S(1)} fusion(bf16[16,64,2048]{2,1,0:T(8,128)(2,1)} %bitcast.44, bf16[16,2048,512]{2,1,0:T(8,128)(2,1)} %param.11), kind=kOutput, calls=%fused_computation.48 | convolution fusion | flops 2147483648 | bytes 39845888 | tf_op jit(solution)/shard_map/ecd,edf->ecf/dot_general | solution.py:28
  91.0 28.2 %convert_bitcast_fusion = bf16[1,16,64,2048]{3,2,1,0:T(8,128)(2,1)} fusion(bf16[16,512,2048]{2,1,0:T(8,128)(2,1)} %param.13, f32[16,64,512]{2,1,0:T(8,128)S(1)} %fusion.19, bf16[16,64,2048]{2,1,0:T(8,128)(2,1)} %bitcast.45, bf16[16,2048,512]{2,1,0:T(8,128)(2,1)} %param.12), kind=kOutput, calls=%fused_computation.6 | convolution fusion | flops 4300210176 | bytes 77594624 | tf_op jit(solution)/shard_map/ecf,efd->ecd/dot_general | solution.py:31
  119.2 103.1 %all-reduce.2.cloned.1.call-done = bf16[1,16,64,2048]{3,2,1,0:T(8,128)(2,1)} async-done(((bf16[1,16,64,2048]{3,2,1,0:T(8,128)(2,1)}), bf16[1,16,64,2048]{3,2,1,0:T(8,128)(2,1)}) %all-reduce.2.cloned.1.call-update) | async-done | bytes 4194320 | tf_op jit(solution)/shard_map/psum | solution.py:49
  222.2 6.5 %copy.42 = bf16[1,16,64,2048]{3,1,0,2:T(8,128)(2,1)} copy(bf16[1,16,64,2048]{3,2,1,0:T(8,128)(2,1)} %all-reduce.2.cloned.1.call-done) | data formatting | bytes 8388608 | tf_op jit(solution)/shard_map/psum | solution.py:49
  228.7 5.2 %all-to-all-start.1 = ((bf16[1,16,64,2048]{3,1,0,2:T(8,128)(2,1)}), bf16[1,16,64,2048]{3,1,0,2:T(8,128)(2,1)}, u32[]{:S(2)}, u32[]{:S(2)}) async-start(bf16[1,16,64,2048]{3,1,0,2:T(8,128)(2,1)} %copy.42), calls=%async_computation.1 | async-start | bytes 8388608 | tf_op jit(solution)/shard_map/all_to_all | solution.py:51
  233.9 0.1 copy.34
  234.0 0.1 reshape.129
  234.1 0.2 fusion.18
  234.3 3.8 %gather_fusion.2 = f32[512]{0:T(512)S(1)} fusion(f32[64,64]{1,0:T(8,128)S(1)} %fusion.18, s32[512]{0:T(512)S(1)} %reshape.129), kind=kCustom, calls=%fused_computation.2 | custom fusion | bytes 8192 | tf_op jit(solution)/shard_map/jit(take_along_axis)/gather | solution.py:17
  238.1 0.1 reshape.132
  238.3 0.1 copy.36
  238.4 43.2 %all-to-all-done.1 = bf16[1,16,64,2048]{3,1,0,2:T(8,128)(2,1)} async-done(((bf16[1,16,64,2048]{3,1,0,2:T(8,128)(2,1)}), bf16[1,16,64,2048]{3,1,0,2:T(8,128)(2,1)}, u32[]{:S(2)}, u32[]{:S(2)}) %all-to-all-start.1) | async-done | bytes 4194336 | tf_op jit(solution)/shard_map/all_to_all | solution.py:51
  281.6 6.5 %copy.43 = bf16[1,16,4,16,2048]{4,3,1,2,0:T(8,128)(2,1)} copy(bf16[1,16,4,16,2048]{4,1,3,2,0:T(8,128)(2,1)} %bitcast.9) | data formatting | bytes 8388608 | tf_op jit(solution)/shard_map/all_to_all | solution.py:51
  288.1 7.2 %gather_fusion.1 = bf16[512,2048]{1,0:T(8,128)(2,1)S(1)} fusion(bf16[1024,2048]{1,0:T(8,128)(2,1)} %bitcast.43, s32[1024]{0:T(1024)S(1)} %pad_clamp_fusion), kind=kCustom, calls=%fused_computation.1 | custom fusion | bytes 4196352 | tf_op jit(solution)/shard_map/gather | solution.py:53
  295.3 1.8 fusion
  297.1 0.8 fusion.4
  (22 shorter events, 0.2 us)
Async XLA Ops:
  6.5 227.6 %copy-start = (bf16[2048,64]{0,1:T(8,128)(2,1)S(1)}, bf16[2048,64]{0,1:T(8,128)(2,1)}, u32[]{:S(2)}) copy-start(bf16[2048,64]{0,1:T(8,128)(2,1)} %param.10) | copy-start | bytes 786436
  6.5 215.7 %all-reduce.2.cloned.1.call-start = ((), (), s32[]{:S(2)}) async-start(), calls=%async_computation.2 | async-start | bytes 8388608 | tf_op jit(solution)/shard_map/psum | solution.py:49
  228.7 5.2 %copy-start.2 = (s32[64,8]{0,1:T(8,128)S(1)}, s32[64,8]{0,1:T(8,128)}, u32[]{:S(2)}) copy-start(s32[64,8]{0,1:T(8,128)} %param.8) | copy-start | bytes 6148
  228.7 52.9 %all-to-all-start.1 = ((bf16[1,16,64,2048]{3,1,0,2:T(8,128)(2,1)}), bf16[1,16,64,2048]{3,1,0,2:T(8,128)(2,1)}, u32[]{:S(2)}, u32[]{:S(2)}) async-start(bf16[1,16,64,2048]{3,1,0,2:T(8,128)(2,1)} %copy.42), calls=%async_computation.1 | async-start | bytes 8388608 | tf_op jit(solution)/shard_map/all_to_all | solution.py:51
  288.1 9.0 %copy-start.1 = (bf16[64,2048]{1,0:T(8,128)(2,1)S(1)}, bf16[64,2048]{1,0:T(8,128)(2,1)}, u32[]{:S(2)}) copy-start(bf16[64,2048]{1,0:T(8,128)(2,1)} %param.7) | copy-start | bytes 786436
Sparse Core Ops, SparseCore 0:
  119.3 102.9 all-reduce.1
where the time goes:
time: 305 us
  waiting for transfers between devices  146 us (48%)
  blocking collectives  52.7 us (17%)
  matrix products  43 us (14%)
  local copies, waits for them, and re-layouts  36.4 us (12%)
  between operations  13.6 us (4%)
  other arithmetic  7.7 us (3%)
  starting transfers between devices  5.17 us (2%)
    psum x1, waiting for transfers between devices, local_block(): full_out = lax.psum(part_out, 'tp')  103 us
    all_to_all x1, blocking collectives, local_block(): recv_buf = lax.all_to_all(send_buf, 'ep', 0, 2, tiled=True)  52.7 us
    all_to_all x1, waiting for transfers between devices, local_block(): back_buf = lax.all_to_all(full_out, 'ep', 2, 0, tiled=True)  43.2 us
    dot_general x1, matrix products, expert_ffn(): jnp.einsum('ecf,efd->ecd', hidden, w_down, preferred_element_type=jnp.flo...  28.2 us
    dot_general x1, matrix products, expert_ffn(): jnp.einsum('ecd,edf->ecf', rows, w_gate, preferred_element_type=jnp.float32)  14.6 us
    gather x1, local copies, waits for them, and re-layouts, local_block(): back_buf[dest_pos].reshape(num_tok, top_k, model_dim).astype(jnp.float32)  7.18 us
    all_to_all x1, local copies, waits for them, and re-layouts, local_block(): back_buf = lax.all_to_all(full_out, 'ep', 2, 0, tiled=True)  6.51 us
    psum x1, local copies, waits for them, and re-layouts, local_block(): full_out = lax.psum(part_out, 'tp')  6.45 us
  transfers between devices with their start and end apart: 2, of which 2 were waited for; matrix products, arithmetic and copies ran while one was open for 1% of the time, Pallas kernels for 0%

commit v1 on v0

v1 whole, which is shorter than its diff:
```python
import functools

import jax
import jax.numpy as jnp
from jax import lax
from jax.experimental import pallas as pl
from jax.experimental.pallas import tpu as pltpu
from jax.sharding import PartitionSpec as P

NORM_EPS = 1e-5
CORES = 2
SLOTS = 12
VMEM_BYTES = 67_043_328
MESH = pl.DeviceIdType.MESH
PIECES = 4
CHUNK = 256
LAG_X = 1
LAG_Y = 4
LAG_O = 7


def split_bf16(val):
    hi = val.astype(jnp.bfloat16)
    rest = val - hi.astype(jnp.float32)
    mid = rest.astype(jnp.bfloat16)
    low = (rest - mid.astype(jnp.float32)).astype(jnp.bfloat16)
    return hi, mid, low


def moe_kernel(tok_hbm, ids_hbm, gain_hbm, wr_hbm, w1_hbm, w3_hbm, w2_hbm, out_ref,
               x_all, ids_all, gain, wr, wbuf, rows, slot_s, gate_s, comb, hid, ybuf, part,
               d_recv, x_send, kept, x_recv, y_recv,
               in_sem, w13_sem, w2_sem, xs_sem, xr_sem, is_sem, ir_sem, ds_sem, dr_sem):
    num_tok, dim = tok_hbm.shape
    top_k = ids_hbm.shape[0]
    num_exp = wr_hbm.shape[0]
    local_exp, kparts = w1_hbm.shape[:2]
    width = w1_hbm.shape[3]
    cap = rows.shape[1] // local_exp
    slots = local_exp * cap
    half_exp = wbuf.shape[1]
    num_chunk = dim // CHUNK
    per_pair = width // CHUNK

    ep = lax.axis_index('ep')
    tp = lax.axis_index('tp')
    core = ep % CORES
    chip = ep // CORES
    mate = {'ep': CORES * chip + 1 - core}
    across = {'ep': CORES * (1 - chip) + core}
    twin = {'tp': 1 - tp}
    b_mate = CORES * chip + 1 - core
    b_across = CORES * (1 - chip) + core
    b_diag = CORES * (1 - chip) + 1 - core

    def w13_copy(e, which):
        src = (w1_hbm, w3_hbm)[which]
        return pltpu.make_async_copy(
            src.at[e], wbuf.at[e % SLOTS, pl.ds(which * kparts, kparts)], w13_sem.at[e, which])

    def w2_copy(j, half):
        col = pl.multiple_of(j * CHUNK, CHUNK)
        sub = pl.multiple_of((j % per_pair) * CHUNK, CHUNK)
        return pltpu.make_async_copy(
            w2_hbm.at[pl.ds(half * half_exp, half_exp), :, pl.ds(col, CHUNK)],
            wbuf.at[SLOTS - num_chunk // per_pair * 2 + (j // per_pair) * 2 + half, :, :, pl.ds(sub, CHUNK)],
            w2_sem.at[j, half])

    own_x = pltpu.make_async_copy(tok_hbm, x_all.at[ep], in_sem.at[0])
    own_ids = pltpu.make_async_copy(ids_hbm, ids_all.at[ep], in_sem.at[1])
    get_wr = pltpu.make_async_copy(wr_hbm, wr, in_sem.at[2])
    get_gain = pltpu.make_async_copy(gain_hbm, gain, in_sem.at[3])
    for copy in (own_x, own_ids, get_gain, get_wr):
        copy.start()
    barrier = pltpu.get_barrier_semaphore()
    for peer in (mate, across, twin):
        pl.semaphore_signal(barrier, inc=1, device_id=peer, device_id_type=MESH)

    def start_w13(e, carry):
        w13_copy(e, 0).start(priority=1)
        w13_copy(e, 1).start(priority=1)
        return carry

    lax.fori_loop(0, SLOTS, start_w13, 0)

    piece = num_tok // PIECES

    def x_part(block, p):
        return x_all.at[block, pl.ds(p * piece, piece)]

    def remote(src, dst, ssem, rsem, peer):
        return pltpu.make_async_remote_copy(
            src_ref=src, dst_ref=dst, send_sem=ssem, recv_sem=rsem, device_id=peer, device_id_type=MESH)

    ids_mate = remote(ids_all.at[ep], ids_all.at[ep], is_sem.at[0], ir_sem.at[0], mate)
    ids_across = remote(ids_all.at[ep], ids_all.at[ep], is_sem.at[1], ir_sem.at[1], across)
    ids_diag = remote(ids_all.at[b_across], ids_all.at[b_across], is_sem.at[2], ir_sem.at[2], mate)
    x_mate = remote(x_all.at[ep], x_all.at[ep], xs_sem.at[2 * PIECES], xr_sem.at[2 * PIECES], mate)
    x_across = [remote(x_part(ep, p), x_part(ep, p), xs_sem.at[p], xr_sem.at[p], across)
                for p in range(PIECES)]
    x_diag = [remote(x_part(b_across, p), x_part(b_across, p), xs_sem.at[PIECES + p], xr_sem.at[PIECES + p], mate)
              for p in range(PIECES)]

    own_ids.wait()
    own_x.wait()
    pl.semaphore_wait(barrier, 3)
    ids_across.start()
    for copy in x_across:
        copy.start()
    ids_mate.start()
    x_mate.start()
    get_gain.wait()
    get_wr.wait()

    def take_block(block):
        tok = x_all[block].astype(jnp.float32)
        inv_rms = lax.rsqrt(jnp.mean(tok * tok, axis=-1, keepdims=True) + NORM_EPS)
        normed = (tok * inv_rms * gain[...].astype(jnp.float32)).astype(jnp.bfloat16)
        logits = lax.dot_general(wr[...], normed, (((1,), (1,)), ((), ())),
                                 preferred_element_type=jnp.float32)
        ids = ids_all[block]
        exp_iota = lax.broadcasted_iota(jnp.int32, (num_exp, num_tok), 0)
        member = exp_iota == ids[0:1, :]
        for k in range(1, top_k):
            member = member | (exp_iota == ids[k:k + 1, :])
        top = jnp.max(jnp.where(member, logits, -jnp.inf), axis=0, keepdims=True)
        weight = jnp.where(member, jnp.exp(jnp.where(member, logits - top, 0.0)), 0.0)
        gate_s[...] = weight / jnp.sum(weight, axis=0, keepdims=True)
        before = (lax.broadcasted_iota(jnp.int32, (num_tok, num_tok), 0)
                  < lax.broadcasted_iota(jnp.int32, (num_tok, num_tok), 1))
        rank = jnp.dot(jnp.where(member, 1.0, 0.0).astype(jnp.bfloat16),
                       jnp.where(before, 1.0, 0.0).astype(jnp.bfloat16), preferred_element_type=jnp.float32)
        slot_s[...] = jnp.where(member, rank, -1.0)
        first = pl.multiple_of(ep * local_exp, local_exp)
        slot_loc = slot_s[pl.ds(first, local_exp), :]
        gate_loc = gate_s[pl.ds(first, local_exp), :]
        slot_iota = lax.broadcasted_iota(jnp.int32, (cap, num_tok), 0).astype(jnp.float32)
        hits = [slot_iota == slot_loc[e:e + 1, :] for e in range(local_exp)]
        pick = jnp.concatenate([jnp.where(hit, 1.0, 0.0) for hit in hits], axis=0)
        rows[block] = jnp.dot(pick.astype(jnp.bfloat16), normed,
                              preferred_element_type=jnp.float32).astype(jnp.bfloat16)
        mix = jnp.concatenate([jnp.where(hits[e], gate_loc[e:e + 1, :], 0.0) for e in range(local_exp)], axis=0)
        comb[block] = jnp.concatenate(split_bf16(mix.T), axis=0)

    take_block(ep)
    ids_mate.wait_recv()
    x_mate.wait_recv()
    take_block(b_mate)
    ids_across.wait_recv()
    ids_diag.start()
    for p in range(PIECES):
        x_across[p].wait_recv()
        x_diag[p].start()
    take_block(b_across)
    ids_diag.wait_recv()
    for p in range(PIECES):
        x_diag[p].wait_recv()
    take_block(b_diag)

    blocks = rows.shape[0]

    def up_step(e, carry):
        w13_copy(e, 0).wait()
        w13_copy(e, 1).wait()
        first = pl.multiple_of(e * cap, cap)
        lhs = jnp.concatenate([rows[b, pl.ds(first, cap), :] for b in range(blocks)], axis=0)
        slot = e % SLOTS
        gate_act = jnp.dot(lhs, wbuf[slot, 0:kparts].reshape(dim, width), preferred_element_type=jnp.float32)
        up_act = jnp.dot(lhs, wbuf[slot, kparts:2 * kparts].reshape(dim, width), preferred_element_type=jnp.float32)
        hid[e] = (jax.nn.silu(gate_act) * up_act).astype(jnp.bfloat16)
        extra = local_exp - SLOTS

        @pl.when(e < extra)
        def _():
            start_w13(e + SLOTS, 0)

        @pl.when((e > extra) & (e < SLOTS) & ((e - extra) % 2 == 1))
        def _():
            for q in range(per_pair):
                for half in range(2):
                    w2_copy((e - extra) // 2 * per_pair + q, half).start(priority=1)

        return carry

    lax.fori_loop(0, local_exp, up_step, 0)

    def d_copy(j):
        return remote(part.at[j, 1 - core], d_recv.at[j], ds_sem.at[0, j], dr_sem.at[0, j], mate)

    def x_copy(j):
        return remote(x_send.at[j], x_recv.at[j], ds_sem.at[1, j], dr_sem.at[1, j], across)

    def y_copy(j):
        return remote(kept.at[j], y_recv.at[j], ds_sem.at[2, j], dr_sem.at[2, j], twin)

    def down_step(j, carry):
        @pl.when(j < num_chunk)
        def _():
            w2_copy(j, 0).wait()
            w2_copy(j, 1).wait()
            base = SLOTS - num_chunk // per_pair * 2 + (j // per_pair) * 2
            sub = pl.multiple_of((j % per_pair) * CHUNK, CHUNK)
            for e in range(local_exp):
                w2 = wbuf[base + e // half_exp, e % half_exp, :, pl.ds(sub, CHUNK)]
                y = jnp.dot(hid[e], w2, preferred_element_type=jnp.float32).astype(jnp.bfloat16)
                for b in range(blocks):
                    ybuf[b, e * cap:(e + 1) * cap, :] = y[b * cap:(b + 1) * cap, :]

            def mix_block(to_core, to_chip):
                block = CORES * to_chip + to_core
                three = jnp.dot(comb[block], ybuf[block], preferred_element_type=jnp.float32)
                part[j, to_core, to_chip] = (three[0:num_tok] + three[num_tok:2 * num_tok]) + three[2 * num_tok:]

            mix_block(1 - core, 0)
            mix_block(1 - core, 1)
            d_copy(j).start()
            mix_block(core, 0)
            mix_block(core, 1)

        @pl.when((j >= LAG_X) & (j < num_chunk + LAG_X))
        def _():
            i = j - LAG_X
            d_copy(i).wait_recv()
            x_send[i] = part[i, core, 1 - chip] + d_recv[i, 1 - chip]
            x_copy(i).start()
            kept[i] = part[i, core, chip] + d_recv[i, chip]

        @pl.when((j >= LAG_Y) & (j < num_chunk + LAG_Y))
        def _():
            i = j - LAG_Y
            x_copy(i).wait_recv()
            kept[i] = kept[i] + x_recv[i]
            y_copy(i).start()

        @pl.when(j >= LAG_O)
        def _():
            i = j - LAG_O
            y_copy(i).wait_recv()
            col = pl.multiple_of(i * CHUNK, CHUNK)
            tok = x_all[ep, :, pl.ds(col, CHUNK)].astype(jnp.float32)
            out_ref[:, pl.ds(col, CHUNK)] = (tok + (kept[i] + y_recv[i])).astype(out_ref.dtype)

        return carry

    lax.fori_loop(0, num_chunk + LAG_O, down_step, 0)

    for copy in (ids_mate, ids_across, ids_diag, x_mate, *x_across, *x_diag):
        copy.wait_send()

    def drain(j, carry):
        d_copy(j).wait_send()
        x_copy(j).wait_send()
        y_copy(j).wait_send()
        return carry

    lax.fori_loop(0, num_chunk, drain, 0)


def moe_call(ep_size, tokens, ids_t, gain, router_t, w_gate, w_up, w_down):
    num_tok, dim = tokens.shape
    top_k = ids_t.shape[0]
    num_exp = router_t.shape[0]
    local_exp, width, _ = w_down.shape
    cap = 2 * top_k * num_tok // num_exp
    kparts = dim // width
    half_exp = local_exp // 2
    chunks = dim // CHUNK
    w_gate = w_gate.reshape(local_exp, kparts, width, width)
    w_up = w_up.reshape(local_exp, kparts, width, width)
    bf16, f32 = jnp.bfloat16, jnp.float32
    vmem = pltpu.VMEM
    dma = pltpu.SemaphoreType.DMA
    any_spec = pl.BlockSpec(memory_space=pl.ANY)
    return pl.pallas_call(
        moe_kernel,
        out_shape=jax.ShapeDtypeStruct((num_tok, dim), tokens.dtype),
        in_specs=[any_spec] * 7,
        out_specs=pl.BlockSpec(memory_space=pltpu.VMEM),
        scratch_shapes=[
            vmem((ep_size, num_tok, dim), bf16),
            vmem((ep_size, top_k, num_tok), jnp.int32),
            vmem((1, dim), bf16),
            vmem((num_exp, dim), bf16),
            vmem((SLOTS, half_exp, width, width), bf16),
            vmem((ep_size, local_exp * cap, dim), bf16),
            vmem((num_exp, num_tok), f32),
            vmem((num_exp, num_tok), f32),
            vmem((ep_size, 3 * num_tok, local_exp * cap), bf16),
            vmem((local_exp, ep_size * cap, width), bf16),
            vmem((ep_size, local_exp * cap, CHUNK), bf16),
            vmem((chunks, CORES, ep_size // CORES, num_tok, CHUNK), f32),
            vmem((chunks, ep_size // CORES, num_tok, CHUNK), f32),
            vmem((chunks, num_tok, CHUNK), f32),
            vmem((chunks, num_tok, CHUNK), f32),
            vmem((chunks, num_tok, CHUNK), f32),
            vmem((chunks, num_tok, CHUNK), f32),
            dma((4,)), dma((local_exp, 2)), dma((chunks, 2)),
            dma((2 * PIECES + 1,)), dma((2 * PIECES + 1,)), dma((3,)), dma((3,)),
            dma((3, chunks)), dma((3, chunks)),
        ],
        compiler_params=pltpu.CompilerParams(
            collective_id=0, has_side_effects=True, vmem_limit_bytes=VMEM_BYTES),
        name='moe_block',
    )(tokens, ids_t, gain, router_t, w_gate, w_up, w_down)


def solution(mesh):
    ep_size = mesh.shape['ep']
    tok_spec = P(('dp', 'ep'), None)

    def local_block(tokens, expert_ids, norm_gain, router_w, w_gate, w_up, w_down):
        return moe_call(ep_size, tokens, expert_ids.T, norm_gain.reshape(1, -1), router_w.T, w_gate, w_up, w_down)

    return jax.shard_map(local_block, mesh=mesh, in_specs=(tok_spec, tok_spec, P(None), P(None, None), P('ep', None, 'tp'), P('ep', None, 'tp'), P('ep', 'tp', None)), out_specs=tok_spec, check_vma=False)
```

time: 305 us -> 51.2 us (0.17)
  waiting for transfers between devices: 146 us -> 0 us
  blocking collectives: 52.7 us -> 0 us
  Pallas kernels: 0 us -> 48.1 us
  matrix products: 43 us -> 0 us
  local copies, waits for them, and re-layouts: 36.4 us -> 2.96 us
  between operations: 13.6 us -> 0.01 us
  other arithmetic: 7.7 us -> 0 us
  starting transfers between devices: 5.17 us -> 0 us
    psum x1 -> x0, waiting for transfers between devices: 103 us -> none  [local_block(): full_out = lax.psum(part_out, 'tp')]
    all_to_all x1 -> x0, blocking collectives: 52.7 us -> none  [local_block(): recv_buf = lax.all_to_all(send_buf, 'ep', 0, 2, tiled=True)]
    pallas_call x0 -> x1, Pallas kernels: none -> 48.1 us  [moe_call(): pl.pallas_call(moe_kernel, out_shape=jax.ShapeDtypeStruct((num_tok, dim),...]
    all_to_all x1 -> x0, waiting for transfers between devices: 43.2 us -> none  [local_block(): back_buf = lax.all_to_all(full_out, 'ep', 2, 0, tiled=True)]
    dot_general x3 -> x0, matrix products: 43 us -> none  [the longest x1 28.2 us: expert_ffn(): jnp.einsum('ecf,efd->ecd', hidden, w_down, preferred_element_type=jnp.flo...]
    gather x7 -> x0, local copies, waits for them, and re-layouts: 17.3 us -> none  [the longest x1 7.18 us: local_block(): back_buf[dest_pos].reshape(num_tok, top_k, model_dim).astype(jnp.float32)]
    all_to_all x2 -> x0, local copies, waits for them, and re-layouts: 8.74 us -> none  [the longest x1 6.51 us: local_block(): back_buf = lax.all_to_all(full_out, 'ep', 2, 0, tiled=True)]
    psum x1 -> x0, local copies, waits for them, and re-layouts: 6.45 us -> none  [local_block(): full_out = lax.psum(part_out, 'tp')]
  transfers between devices with their start and end apart: 2 -> 0, of which waited for: 2 -> 0; matrix products, arithmetic and copies ran while one was open for 1% -> 0% of each run, Pallas kernels for 0% -> 0%
where the time goes in v1:
time: 51.2 us; the launch traced here: 51.1 us
  Pallas kernels  48.1 us (94%)
  local copies, waits for them, and re-layouts  2.96 us (6%)
    pallas_call x1, Pallas kernels, moe_call(): pl.pallas_call(moe_kernel, out_shape=jax.ShapeDtypeStruct((num_tok, dim),...  48.1 us
    unnamed x1, local copies, waits for them, and re-layouts  1.67 us
    reshape x1, local copies, waits for them, and re-layouts, local_block(): norm_gain.reshape(1, -1)  1.29 us

profile of v1, /device:TPU:0, one launch (start us, length us, event | category | flops | bytes accessed | tf_op | source)
XLA Modules:
  0.0 51.1 jit_solution(12454157152031150242)
XLA Ops:
  0.0 1.3 %reshape.9.gain_hbm = bf16[1,2048]{1,0:T(2,128)(2,1)} reshape(bf16[2048]{0:T(1024)(128)(2,1)} %param.9) | data formatting | bytes 8192 | tf_op jit(solution)/shard_map/reshape | solution.py:312
  1.3 48.1 %moe_block.1 = bf16[64,2048]{1,0:T(8,128)(2,1)} custom-call(bf16[64,2048]{1,0:T(8,128)(2,1)} %tok_hbm.1, s32[8,64]{1,0:T(8,128)} %bitcast.7, bf16[1,2048]{1,0:T(2,128)(2,1)} %reshape.9.gain_hbm, bf16[64,2048]{1,0:T(8,128)(2,1)} %bitcast.6, bf16[16,4,512,512]{3,2,1,0:T(8,128)(2,1)} %bitcast.4, bf16[16,4,512,512]{3,2,1,0:T(8,128)(2,1)} %bitcast.5, ...), custom_call_target="tpu_custom_call" | custom-call | tf_op jit(solution)/shard_map/moe_block/pallas_call | solution.py:274
  49.4 1.7 %copy.9 = bf16[64,2048]{1,0:T(8,128)(2,1)} copy(bf16[64,2048]{1,0:T(8,128)(2,1)} %moe_block.1) | data formatting | bytes 524288

commit v2 on v1

v2 whole, which is shorter than its diff:
```python
import jax
import jax.numpy as jnp
from jax import lax
from jax.experimental import pallas as pl
from jax.experimental.pallas import tpu as pltpu
from jax.sharding import PartitionSpec as P

NORM_EPS = 1e-5
CORES = 2
SLOTS = 11
VMEM_BYTES = 63 * 2**20
MESH = pl.DeviceIdType.MESH
PIECE = 8
DIRECT = 6
CHUNK = 256
PARTS = 2
GROUP = 4
LAG_X = 1
LAG_Y = 4
LAG_O = 8


def split_bf16(val):
    hi = val.astype(jnp.bfloat16)
    rest = val - hi.astype(jnp.float32)
    mid = rest.astype(jnp.bfloat16)
    low = (rest - mid.astype(jnp.float32)).astype(jnp.bfloat16)
    return hi, mid, low


def moe_kernel(tok_hbm, ids_hbm, gain_hbm, wr_hbm, w1_hbm, w3_hbm, w2_hbm, out_ref,
               x_all, ids_all, gain, wr, wbuf, normed, rows, slot_s, gate_s, pick, comb, hid, ybuf, part,
               d_recv, x_send, kept, x_recv, y_recv,
               in_sem, w_sem, xa_rs, xt_rs, xd_rs, xm_rs, ir_sem, dr_sem, xr_sem, yr_sem, send_sem):
    num_tok, dim = tok_hbm.shape
    top_k = ids_hbm.shape[0]
    num_exp = wr_hbm.shape[0]
    local_exp, kparts = w1_hbm.shape[:2]
    width = w1_hbm.shape[3]
    blocks = rows.shape[0]
    cap = rows.shape[1] // local_exp
    half_exp = wbuf.shape[1]
    num_chunk = dim // CHUNK
    per_pair = width // CHUNK
    extra = local_exp - SLOTS
    scope = jax.named_scope

    ep = lax.axis_index('ep')
    tp = lax.axis_index('tp')
    core = ep % CORES
    chip = ep // CORES
    b_mate = CORES * chip + 1 - core
    b_across = CORES * (1 - chip) + core
    b_diag = CORES * (1 - chip) + 1 - core
    mate = {'ep': b_mate}
    across = {'ep': b_across}
    twin = {'tp': 1 - tp}

    def w13_copy(e, which):
        src = (w1_hbm, w3_hbm)[which]
        return pltpu.make_async_copy(
            src.at[e], wbuf.at[e % SLOTS, pl.ds(which * kparts, kparts)], w_sem.at[e % SLOTS])

    def w2_slot(j, half):
        return (extra + (j // per_pair) * 2 + half) % SLOTS

    def w2_copy(j, half):
        col = pl.multiple_of(j * CHUNK, CHUNK)
        sub = pl.multiple_of((j % per_pair) * CHUNK, CHUNK)
        return pltpu.make_async_copy(
            w2_hbm.at[pl.ds(half * half_exp, half_exp), :, pl.ds(col, CHUNK)],
            wbuf.at[w2_slot(j, half), :, :, pl.ds(sub, CHUNK)], w_sem.at[w2_slot(j, j % per_pair)])

    def w_wait(slot):
        pltpu.make_async_copy(wbuf.at[slot], wbuf.at[slot], w_sem.at[slot]).wait()

    own_x = pltpu.make_async_copy(tok_hbm, x_all.at[ep], in_sem.at[0])
    own_ids = pltpu.make_async_copy(ids_hbm, ids_all.at[ep], in_sem.at[1])
    get_wr = pltpu.make_async_copy(wr_hbm, wr, in_sem.at[2])
    get_gain = pltpu.make_async_copy(gain_hbm, gain, in_sem.at[3])
    for copy in (own_x, own_ids, get_gain, get_wr):
        copy.start()
    barrier = pltpu.get_barrier_semaphore()
    for peer in (mate, across, twin):
        pl.semaphore_signal(barrier, inc=1, device_id=peer, device_id_type=MESH)

    def start_w13(e, carry):
        w13_copy(e, 0).start(priority=1)
        w13_copy(e, 1).start(priority=1)
        return carry

    lax.fori_loop(0, SLOTS, start_w13, 0)

    def remote(src, dst, ssem, rsem, peer):
        return pltpu.make_async_remote_copy(
            src_ref=src, dst_ref=dst, send_sem=ssem, recv_sem=rsem, device_id=peer, device_id_type=MESH)

    pieces = num_tok // PIECE

    def x_part(block, k, side):
        first = pl.multiple_of((k + side * (pieces - 1 - 2 * k)) * PIECE, PIECE)
        return x_all.at[block, pl.ds(first, PIECE)]

    def same(ref, ssem, rsem, peer):
        return remote(ref, ref, ssem, rsem, peer)

    swapped = pieces - DIRECT
    ids_mate = same(ids_all.at[ep], send_sem.at[0], ir_sem.at[0], mate)
    ids_across = same(ids_all.at[ep], send_sem.at[0], ir_sem.at[1], across)
    ids_diag = same(ids_all.at[b_across], send_sem.at[0], ir_sem.at[2], mate)
    x_mate = same(x_all.at[ep], send_sem.at[1], xm_rs.at[0], mate)
    x_across = [same(x_part(ep, k, tp), send_sem.at[2], xa_rs.at[k], across) for k in range(DIRECT)]
    x_twin = [same(x_part(b_across, k, tp), send_sem.at[3], xt_rs.at[k], twin) for k in range(swapped)]
    x_diag = [same(x_part(b_across, k, tp), send_sem.at[4], xd_rs.at[0], mate) for k in range(pieces)]
    all_ids = same(ids_all.at[pl.ds(0, 3)], send_sem.at[0], ir_sem.at[0], mate)
    all_across = same(x_all.at[0, pl.ds(0, DIRECT * PIECE)], send_sem.at[2], xa_rs.at[0], across)
    all_twin = same(x_all.at[0, pl.ds(0, swapped * PIECE)], send_sem.at[3], xt_rs.at[0], twin)
    all_diag = same(x_all.at[b_diag], send_sem.at[4], xd_rs.at[0], mate)

    with scope('wait_own'):
        own_ids.wait()
        own_x.wait()
    with scope('wait_barrier'):
        pl.semaphore_wait(barrier, 3)
    ids_across.start()
    for copy in x_across:
        copy.start()
    ids_mate.start()
    x_mate.start()
    get_gain.wait()
    get_wr.wait()

    def route(block):
        ids = ids_all[block]
        exp_iota = lax.broadcasted_iota(jnp.int32, (num_exp, num_tok), 0)
        member = exp_iota == ids[0:1, :]
        for k in range(1, top_k):
            member = member | (exp_iota == ids[k:k + 1, :])
        before = (lax.broadcasted_iota(jnp.int32, (num_tok, num_tok), 0)
                  < lax.broadcasted_iota(jnp.int32, (num_tok, num_tok), 1))
        rank = jnp.dot(jnp.where(member, 1.0, 0.0).astype(jnp.bfloat16),
                       jnp.where(before, 1.0, 0.0).astype(jnp.bfloat16), preferred_element_type=jnp.float32)
        slot_s[block] = jnp.where(member, rank, -1.0)
        first = pl.multiple_of(ep * local_exp, local_exp)
        slot_loc = slot_s[block, pl.ds(first, local_exp), :]
        slot_iota = lax.broadcasted_iota(jnp.int32, (cap, num_tok), 0).astype(jnp.float32)
        pick[block] = jnp.concatenate(
            [jnp.where(slot_iota == slot_loc[e:e + 1, :], 1.0, 0.0) for e in range(local_exp)],
            axis=0).astype(jnp.bfloat16)

    def norm_rows(block):
        tok = x_all[block].astype(jnp.float32)
        inv_rms = lax.rsqrt(jnp.mean(tok * tok, axis=-1, keepdims=True) + NORM_EPS)
        scale = gain[...].astype(jnp.float32)
        scale = jnp.concatenate([scale[r:r + 1] for r in range(scale.shape[0])], axis=1)
        norm = (tok * inv_rms * scale).astype(jnp.bfloat16)
        normed[block] = norm

    def gather(block):
        rows[block] = jnp.dot(pick[block], normed[block], preferred_element_type=jnp.float32).astype(jnp.bfloat16)

    def gates(block):
        logits = lax.dot_general(wr[...], normed[block], (((1,), (1,)), ((), ())),
                                 preferred_element_type=jnp.float32)
        member = slot_s[block] >= 0.0
        top = jnp.max(jnp.where(member, logits, -jnp.inf), axis=0, keepdims=True)
        weight = jnp.where(member, jnp.exp(jnp.where(member, logits - top, 0.0)), 0.0)
        gate_s[...] = weight / jnp.sum(weight, axis=0, keepdims=True)
        first = pl.multiple_of(ep * local_exp, local_exp)
        gate_loc = gate_s[pl.ds(first, local_exp), :]
        spread = jnp.concatenate(
            [jnp.broadcast_to(gate_loc[e:e + 1, :], (cap, num_tok)) for e in range(local_exp)], axis=0)
        mix = jnp.where(pick[block].astype(jnp.float32) > 0.0, spread, 0.0)
        comb[block] = jnp.concatenate(split_bf16(mix.T), axis=0)

    with scope('own'):
        route(ep)
        norm_rows(ep)
        gather(ep)
    with scope('wait_mate'):
        ids_mate.wait_recv()
    with scope('mate'):
        route(b_mate)
        x_mate.wait_recv()
        norm_rows(b_mate)
        gather(b_mate)
        gates(ep)
        gates(b_mate)
    with scope('route_across'):
        ids_across.wait_recv()
        ids_diag.start()
        route(b_across)

    def relay(k):
        x_across[k].wait_recv()
        if k < swapped:
            x_twin[k].start()
        x_diag[k].start()

    def from_twin(k):
        x_twin[k].wait_recv()
        x_diag[pieces - 1 - k].start()

    with scope('relay'):
        for k in range(DIRECT - swapped):
            relay(k)
    with scope('route_diag'):
        ids_diag.wait_recv()
        route(b_diag)
    with scope('relay'):
        for k in range(DIRECT - swapped, DIRECT):
            from_twin(k - DIRECT + swapped)
            relay(k)
    with scope('norm_across'):
        norm_rows(b_across)
    with scope('wait_diag'):
        all_diag.wait_recv()
    with scope('gather_rest'):
        norm_rows(b_diag)
        gather(b_across)
        gather(b_diag)

    def up_one(e):
        first = pl.multiple_of(e * cap, cap)
        count = blocks * cap
        lhs = jnp.concatenate([rows[b % blocks, pl.ds(first, cap), :] for b in range(2 * blocks)], axis=0)
        slot = e % SLOTS
        gate_act = jnp.dot(lhs, wbuf[slot, 0:kparts].reshape(dim, width), preferred_element_type=jnp.float32)
        up_act = jnp.dot(lhs, wbuf[slot, kparts:2 * kparts].reshape(dim, width), preferred_element_type=jnp.float32)
        hid[e] = (jax.nn.silu(gate_act[0:count]) * up_act[0:count]).astype(jnp.bfloat16)

    def refill(e):
        @pl.when(e < extra)
        def _():
            start_w13(e + SLOTS, 0)

        @pl.when((e > extra) & (e < extra + 2 * num_chunk // per_pair) & ((e - extra) % 2 == 1))
        def _():
            for q in range(per_pair):
                for half in range(2):
                    w2_copy((e - extra) // 2 * per_pair + q, half).start(priority=1)

    def up_step(group):
        def step(i, carry):
            with scope('up_wait'):
                for u in range(group):
                    w_wait((i * group + u) % SLOTS)
            for u in range(group):
                up_one(i * group + u)
            for u in range(group):
                refill(i * group + u)
            return carry
        return step

    early = local_exp // 4 * 3
    lax.fori_loop(0, early // GROUP, up_step(GROUP), 0)
    with scope('gates_rest'):
        gates(b_across)
        gates(b_diag)
    lax.fori_loop(early, local_exp, up_step(1), 0)
    for copy in (all_ids, x_mate, all_across, all_twin, all_diag):
        copy.wait_send()

    def d_copy(j):
        return remote(part.at[j, 1 - core], d_recv.at[j], send_sem.at[5], dr_sem.at[j], mate)

    part_rows = num_tok // PARTS

    def x_copy(j, r):
        span = pl.ds(r * part_rows, part_rows)
        return remote(x_send.at[j, span], x_recv.at[j, span], send_sem.at[6], xr_sem.at[j, r], across)

    def y_copy(j, r):
        span = pl.ds(r * part_rows, part_rows)
        return remote(kept.at[j, span], y_recv.at[j, span], send_sem.at[7], yr_sem.at[j, r], twin)

    def down(j):
        with scope('down_wait'):
            w_wait(w2_slot(j, j % per_pair))
        sub = pl.multiple_of((j % per_pair) * CHUNK, CHUNK)
        for e in range(local_exp):
            w2 = wbuf[w2_slot(j, e // half_exp), e % half_exp, :, pl.ds(sub, CHUNK)]
            lhs = jnp.concatenate([hid[e], hid[e]], axis=0)
            y = jnp.dot(lhs, w2, preferred_element_type=jnp.float32).astype(jnp.bfloat16)
            for b in range(blocks):
                ybuf[b, e * cap:(e + 1) * cap, :] = y[b * cap:(b + 1) * cap, :]

        def mix_block(to_core, to_chip):
            block = CORES * to_chip + to_core
            three = jnp.dot(comb[block], ybuf[block], preferred_element_type=jnp.float32)
            part[j, to_core, to_chip] = (three[0:num_tok] + three[num_tok:2 * num_tok]) + three[2 * num_tok:]

        mix_block(1 - core, 0)
        mix_block(1 - core, 1)
        d_copy(j).start()
        mix_block(core, 0)
        mix_block(core, 1)

    def to_across(i):
        with scope('d_wait'):
            d_copy(i).wait_recv()
        for r in range(PARTS):
            span = pl.ds(r * part_rows, part_rows)
            x_send[i, span] = part[i, core, 1 - chip, span] + d_recv[i, 1 - chip, span]
            x_copy(i, r).start()
        kept[i] = part[i, core, chip] + d_recv[i, chip]

    def to_twin(i):
        for r in range(PARTS):
            with scope('x_wait'):
                x_copy(i, r).wait_recv()
            span = pl.ds(r * part_rows, part_rows)
            kept[i, span] = kept[i, span] + x_recv[i, span]
            y_copy(i, r).start()

    def finish(i):
        with scope('y_wait'):
            for r in range(PARTS):
                y_copy(i, r).wait_recv()
        col = pl.multiple_of(i * CHUNK, CHUNK)
        tok = x_all[ep, :, pl.ds(col, CHUNK)].astype(jnp.float32)
        out_ref[:, pl.ds(col, CHUNK)] = (tok + (kept[i] + y_recv[i])).astype(out_ref.dtype)

    def down_step(j, carry):
        @pl.when(j < num_chunk)
        def _():
            down(j)

        @pl.when((j >= LAG_X) & (j < num_chunk + LAG_X))
        def _():
            to_across(j - LAG_X)

        @pl.when((j >= LAG_Y) & (j < num_chunk + LAG_Y))
        def _():
            to_twin(j - LAG_Y)

        @pl.when(j >= LAG_O)
        def _():
            finish(j - LAG_O)

        return carry

    lax.fori_loop(0, num_chunk + LAG_O, down_step, 0)
    remote(d_recv, d_recv, send_sem.at[5], dr_sem.at[0], mate).wait_send()
    remote(x_send, x_recv, send_sem.at[6], xr_sem.at[0, 0], across).wait_send()
    remote(kept, y_recv, send_sem.at[7], yr_sem.at[0, 0], twin).wait_send()


def moe_call(ep_size, tokens, ids_t, gain, router_t, w_gate, w_up, w_down):
    num_tok, dim = tokens.shape
    top_k = ids_t.shape[0]
    num_exp = router_t.shape[0]
    local_exp, width, _ = w_down.shape
    cap = 2 * top_k * num_tok // num_exp
    kparts = dim // width
    half_exp = local_exp // 2
    chunks = dim // CHUNK
    pieces = num_tok // PIECE
    w_gate = w_gate.reshape(local_exp, kparts, width, width)
    w_up = w_up.reshape(local_exp, kparts, width, width)
    bf16, f32 = jnp.bfloat16, jnp.float32
    vmem = pltpu.VMEM
    dma = pltpu.SemaphoreType.DMA
    any_spec = pl.BlockSpec(memory_space=pl.ANY)
    return pl.pallas_call(
        moe_kernel,
        out_shape=pltpu.VMEM((num_tok, dim), tokens.dtype),
        in_specs=[any_spec] * 7,
        out_specs=pl.BlockSpec(memory_space=pltpu.VMEM),
        scratch_shapes=[
            vmem((ep_size, num_tok, dim), bf16),
            vmem((ep_size, top_k, num_tok), jnp.int32),
            vmem(gain.shape, bf16),
            vmem((num_exp, dim), bf16),
            vmem((SLOTS, half_exp, width, width), bf16),
            vmem((ep_size, num_tok, dim), bf16),
            vmem((ep_size, local_exp * cap, dim), bf16),
            vmem((ep_size, num_exp, num_tok), f32),
            vmem((num_exp, num_tok), f32),
            vmem((ep_size, local_exp * cap, num_tok), bf16),
            vmem((ep_size, 3 * num_tok, local_exp * cap), bf16),
            vmem((local_exp, ep_size * cap, width), bf16),
            vmem((ep_size, local_exp * cap, CHUNK), bf16),
            vmem((chunks, CORES, ep_size // CORES, num_tok, CHUNK), f32),
            vmem((chunks, ep_size // CORES, num_tok, CHUNK), f32),
            vmem((chunks, num_tok, CHUNK), f32),
            vmem((chunks, num_tok, CHUNK), f32),
            vmem((chunks, num_tok, CHUNK), f32),
            vmem((chunks, num_tok, CHUNK), f32),
            dma((4,)), dma((SLOTS,)), dma((DIRECT,)), dma((pieces - DIRECT,)), dma((1,)), dma((1,)), dma((3,)),
            dma((chunks,)), dma((chunks, PARTS)), dma((chunks, PARTS)), dma((8,)),
        ],
        compiler_params=pltpu.CompilerParams(
            collective_id=0, has_side_effects=True, vmem_limit_bytes=VMEM_BYTES),
        name='moe_block',
    )(tokens, ids_t, gain, router_t, w_gate, w_up, w_down)


def solution(mesh):
    ep_size = mesh.shape['ep']
    tok_spec = P(('dp', 'ep'), None)

    def local_block(tokens, expert_ids, norm_gain, router_w, w_gate, w_up, w_down):
        return moe_call(ep_size, tokens, expert_ids.T, norm_gain.reshape(-1, 128), router_w.T, w_gate, w_up, w_down)

    return jax.shard_map(local_block, mesh=mesh, in_specs=(tok_spec, tok_spec, P(None), P(None, None), P('ep', None, 'tp'), P('ep', None, 'tp'), P('ep', 'tp', None)), out_specs=tok_spec, check_vma=False)
```

time: 51.2 us -> 45 us (0.88)
  Pallas kernels: 48.1 us -> 44.2 us
  local copies, waits for them, and re-layouts: 2.96 us -> 0.71 us
    pallas_call x1, Pallas kernels: 48.1 us -> 44.2 us  [moe_call(): pl.pallas_call(moe_kernel, out_shape=pltpu.VMEM((num_tok, dim), tokens.dt...]
    reshape x1 -> x0, local copies, waits for them, and re-layouts: 1.29 us -> none  [local_block(): norm_gain.reshape(1, -1)]
    unnamed x1, local copies, waits for them, and re-layouts: 1.67 us -> 0.71 us
where the time goes in v2:
time: 45 us; the launch traced here: 44.9 us
  Pallas kernels  44.2 us (98%)
  local copies, waits for them, and re-layouts  0.71 us (2%)
    pallas_call x1, Pallas kernels, moe_call(): pl.pallas_call(moe_kernel, out_shape=pltpu.VMEM((num_tok, dim), tokens.dt...  44.2 us

profile of v2, /device:TPU:0, one launch (start us, length us, event | category | flops | bytes accessed | tf_op | source)
XLA Modules:
  0.0 44.9 jit_solution(14689055876427946015)
XLA Ops:
  0.0 44.2 %moe_block.1 = bf16[64,2048]{1,0:T(8,128)(2,1)S(1)} custom-call(bf16[64,2048]{1,0:T(8,128)(2,1)} %tok_hbm.1, s32[8,64]{1,0:T(8,128)} %bitcast.8, bf16[16,128]{1,0:T(8,128)(2,1)} %bitcast.9, bf16[64,2048]{1,0:T(8,128)(2,1)} %bitcast.7, bf16[16,4,512,512]{3,2,1,0:T(8,128)(2,1)} %bitcast.5, bf16[16,4,512,512]{3,2,1,0:T(8,128)(2,1)} %bitcast.6, ...), custom_call_target="tpu_custom_call" | custom-call | tf_op jit(solution)/shard_map/moe_block/pallas_call | solution.py:365
  44.2 0.7 %copy.9 = bf16[64,2048]{1,0:T(8,128)(2,1)} copy(bf16[64,2048]{1,0:T(8,128)(2,1)S(1)} %moe_block.1) | data formatting | bytes 524288

commit v3 on v2

--- a/solution.py
+++ b/solution.py
@@ -1,3 +1,5 @@
+import functools
+
 import jax
 import jax.numpy as jnp
 from jax import lax
@@ -252,12 +254,13 @@
             return carry
         return step
 
-    early = local_exp // 4 * 3
-    lax.fori_loop(0, early // GROUP, up_step(GROUP), 0)
+    fours, pairs = local_exp // 2, local_exp // 4 * 3
+    lax.fori_loop(0, fours // 4, up_step(4), 0)
+    lax.fori_loop(fours // 2, pairs // 2, up_step(2), 0)
     with scope('gates_rest'):
         gates(b_across)
         gates(b_diag)
-    lax.fori_loop(early, local_exp, up_step(1), 0)
+    lax.fori_loop(pairs, local_exp, up_step(1), 0)
     for copy in (all_ids, x_mate, all_across, all_twin, all_diag):
         copy.wait_send()
 
@@ -272,7 +275,7 @@
 
     def y_copy(j, r):
         span = pl.ds(r * part_rows, part_rows)
-        return remote(kept.at[j, span], y_recv.at[j, span], send_sem.at[7], yr_sem.at[j, r], twin)
+        return remote(kept.at[j, span], y_recv.at[j, span], send_sem.at[7], yr_sem.at[j], twin)
 
     def down(j):
         with scope('down_wait'):
@@ -315,8 +318,7 @@
 
     def finish(i):
         with scope('y_wait'):
-            for r in range(PARTS):
-                y_copy(i, r).wait_recv()
+            remote(kept.at[i], y_recv.at[i], send_sem.at[7], yr_sem.at[i], twin).wait_recv()
         col = pl.multiple_of(i * CHUNK, CHUNK)
         tok = x_all[ep, :, pl.ds(col, CHUNK)].astype(jnp.float32)
         out_ref[:, pl.ds(col, CHUNK)] = (tok + (kept[i] + y_recv[i])).astype(out_ref.dtype)
@@ -343,7 +345,11 @@
     lax.fori_loop(0, num_chunk + LAG_O, down_step, 0)
     remote(d_recv, d_recv, send_sem.at[5], dr_sem.at[0], mate).wait_send()
     remote(x_send, x_recv, send_sem.at[6], xr_sem.at[0, 0], across).wait_send()
-    remote(kept, y_recv, send_sem.at[7], yr_sem.at[0, 0], twin).wait_send()
+    remote(kept, y_recv, send_sem.at[7], yr_sem.at[0], twin).wait_send()
+
+
+def scoped_kernel(sems, *refs):
+    pl.run_scoped(lambda *held: moe_kernel(*refs, *held), *sems)
 
 
 def moe_call(ep_size, tokens, ids_t, gain, router_t, w_gate, w_up, w_down):
@@ -362,8 +368,12 @@
     vmem = pltpu.VMEM
     dma = pltpu.SemaphoreType.DMA
     any_spec = pl.BlockSpec(memory_space=pl.ANY)
+    sems = (
+        dma((4,)), dma((SLOTS,)), dma((DIRECT,)), dma((pieces - DIRECT,)), dma((1,)), dma((1,)), dma((3,)),
+        dma((chunks,)), dma((chunks, PARTS)), dma((chunks,)), dma((8,)),
+    )
     return pl.pallas_call(
-        moe_kernel,
+        functools.partial(scoped_kernel, sems),
         out_shape=pltpu.VMEM((num_tok, dim), tokens.dtype),
         in_specs=[any_spec] * 7,
         out_specs=pl.BlockSpec(memory_space=pltpu.VMEM),
@@ -387,8 +397,6 @@
             vmem((chunks, num_tok, CHUNK), f32),
             vmem((chunks, num_tok, CHUNK), f32),
             vmem((chunks, num_tok, CHUNK), f32),
-            dma((4,)), dma((SLOTS,)), dma((DIRECT,)), dma((pieces - DIRECT,)), dma((1,)), dma((1,)), dma((3,)),
-            dma((chunks,)), dma((chunks, PARTS)), dma((chunks, PARTS)), dma((8,)),
         ],
         compiler_params=pltpu.CompilerParams(
             collective_id=0, has_side_effects=True, vmem_limit_bytes=VMEM_BYTES),

time: 45 us -> 44.3 us (0.984)
  Pallas kernels: 44.2 us -> 43.5 us
    pallas_call x1, Pallas kernels: 44.2 us -> 43.5 us  [moe_call(): pl.pallas_call(functools.partial(scoped_kernel, sems), out_shape=pltpu.VM...]
where the time goes in v3:
time: 44.3 us; the launch traced here: 44.2 us
  Pallas kernels  43.5 us (98%)
  local copies, waits for them, and re-layouts  0.71 us (2%)
    pallas_call x1, Pallas kernels, moe_call(): pl.pallas_call(functools.partial(scoped_kernel, sems), out_shape=pltpu.VM...  43.5 us

profile of v3, /device:TPU:0, one launch (start us, length us, event | category | flops | bytes accessed | tf_op | source)
XLA Modules:
  0.0 44.2 jit_solution(879205117318446228)
XLA Ops:
  0.0 43.5 %moe_block.1 = bf16[64,2048]{1,0:T(8,128)(2,1)S(1)} custom-call(bf16[64,2048]{1,0:T(8,128)(2,1)} %refs_0_.1, s32[8,64]{1,0:T(8,128)} %bitcast.8, bf16[16,128]{1,0:T(8,128)(2,1)} %bitcast.9, bf16[64,2048]{1,0:T(8,128)(2,1)} %bitcast.7, bf16[16,4,512,512]{3,2,1,0:T(8,128)(2,1)} %bitcast.5, bf16[16,4,512,512]{3,2,1,0:T(8,128)(2,1)} %bitcast.6, ...), custom_call_target="tpu_custom_call" | custom-call | tf_op jit(solution)/shard_map/moe_block/pallas_call | solution.py:375
  43.5 0.7 %copy.9 = bf16[64,2048]{1,0:T(8,128)(2,1)} copy(bf16[64,2048]{1,0:T(8,128)(2,1)S(1)} %moe_block.1) | data formatting | bytes 524288

commit v4 on v3

--- a/solution.py
+++ b/solution.py
@@ -15,7 +15,7 @@
 PIECE = 8
 DIRECT = 6
 CHUNK = 256
-PARTS = 2
+PARTS = 4
 GROUP = 4
 LAG_X = 1
 LAG_Y = 4
@@ -295,9 +295,9 @@
 
         mix_block(1 - core, 0)
         mix_block(1 - core, 1)
-        d_copy(j).start()
         mix_block(core, 0)
         mix_block(core, 1)
+        d_copy(j).start()
 
     def to_across(i):
         with scope('d_wait'):

time: 44.3 us -> 44.1 us (level)
  no operation moved by 1% of the time
where the time goes in v4:
time: 44.1 us; the launch traced here: 44 us
  Pallas kernels  43.3 us (98%)
  local copies, waits for them, and re-layouts  0.71 us (2%)
    pallas_call x1, Pallas kernels, moe_call(): pl.pallas_call(functools.partial(scoped_kernel, sems), out_shape=pltpu.VM...  43.3 us

profile of v4, /device:TPU:0, one launch (start us, length us, event | category | flops | bytes accessed | tf_op | source)
XLA Modules:
  0.0 44.0 jit_solution(11455097715753003218)
XLA Ops:
  0.0 43.3 %moe_block.1 = bf16[64,2048]{1,0:T(8,128)(2,1)S(1)} custom-call(bf16[64,2048]{1,0:T(8,128)(2,1)} %refs_0_.1, s32[8,64]{1,0:T(8,128)} %bitcast.8, bf16[16,128]{1,0:T(8,128)(2,1)} %bitcast.9, bf16[64,2048]{1,0:T(8,128)(2,1)} %bitcast.7, bf16[16,4,512,512]{3,2,1,0:T(8,128)(2,1)} %bitcast.5, bf16[16,4,512,512]{3,2,1,0:T(8,128)(2,1)} %bitcast.6, ...), custom_call_target="tpu_custom_call" | custom-call | tf_op jit(solution)/shard_map/moe_block/pallas_call | solution.py:375
  43.3 0.7 %copy.9 = bf16[64,2048]{1,0:T(8,128)(2,1)} copy(bf16[64,2048]{1,0:T(8,128)(2,1)S(1)} %moe_block.1) | data formatting | bytes 524288
